TPU v7x, 32 devices: a whole 2x2x4 slice. The times are simulated.
32 devices in a mesh: gx: 4 (over z), gy: 4 (over x, core), gz: 2 (over y).
Axes of the slice: x: 2, y: 2, z: 4, core: 2. Of those that a mesh axis runs over, the one named last changes fastest.
Arguments:
- blocks: bfloat16 [4, 4, 128, 256, 256], P('gy', 'gx'), may hold values from -0.0625 to 0.0625
- block_rows: int32 [4, 4, 128], P('gy', 'gx'), may hold values from 0 to 15
- block_cols: int32 [4, 4, 128], P('gy', 'gx'), may hold values from 0 to 15
- probe_bits: int32 [16384, 256], P(('gy', 'gx'), 'gz'), may hold values from 0 to 1
- shift: float32 [16384], P(('gy', 'gx')), may hold values from 0 to 0.7
Outputs:
- forms: float32 [3, 256], P(None, 'gz')
- last_term: float32 [16384, 256], P(('gy', 'gx'), 'gz')
All inputs are finite; a program needn't handle non-finite values.
Results may differ from a plain program's by a relative error of at most 0.02.
Values may be sent and summed in bfloat16 or wider, within the bound.
No kernel may reach another device: no remote copies, remote signals or barrier semaphores. Data moves between devices by JAX's collectives and lax.ppermute only.
A program may use at most 128 MiB of HBM per device.

v0:
```python
import jax
import jax.numpy as jnp
from jax import lax
from jax.sharding import PartitionSpec as P


def body(blocks, block_rows, block_cols, probe_bits, shift):
    tile_blocks = blocks[0, 0]
    rows_here = block_rows[0, 0]
    cols_here = block_cols[0, 0]
    block_size = tile_blocks.shape[1]
    local_rows = shift.shape[0]
    probe_count = probe_bits.shape[1]
    tile_rows = local_rows // block_size * lax.axis_size("gx")
    signs = (2 * probe_bits - 1).astype(jnp.float32)

    def apply_operator(field):
        rounded = field.astype(jnp.bfloat16)
        whole = lax.all_gather(rounded, "gy", axis=0, tiled=True)
        whole = whole.reshape(whole.shape[0] // block_size, block_size, probe_count)
        picked = whole[cols_here]
        product = jnp.einsum(
            "kab,kbp->kap", tile_blocks, picked, preferred_element_type=jnp.float32
        )
        partial_rows = (
            jnp.zeros((tile_rows, block_size, probe_count), jnp.float32).at[rows_here].add(product)
        )
        summed = lax.psum_scatter(
            partial_rows.reshape(lax.axis_size("gx") * local_rows, probe_count).astype(
                jnp.bfloat16
            ),
            "gx",
            scatter_dimension=0,
            tiled=True,
        ).astype(jnp.float32)
        return summed + shift[:, None] * field

    first = apply_operator(signs)
    second = 2.0 * apply_operator(first) - signs
    third = 2.0 * apply_operator(second) - first
    forms = jnp.stack(
        [lax.psum(jnp.sum(signs * term, axis=0), ("gx", "gy")) for term in (first, second, third)]
    )
    return (forms, third)


def solution(mesh):
    return jax.shard_map(
        body,
        mesh=mesh,
        in_specs=(
            P("gy", "gx", None, None, None),
            P("gy", "gx", None),
            P("gy", "gx", None),
            P(("gy", "gx"), "gz"),
            P(("gy", "gx")),
        ),
        out_specs=(P(None, "gz"), P(("gy", "gx"), "gz")),
        check_vma=False,
    )
```

profile of v0, /device:TPU:0, one launch (start us, length us, event | category | flops | bytes accessed | tf_op | source)
XLA Modules:
  0.0 390.7 jit_solution(4236453247020909070)
XLA Ops:
  7.2 0.0 all-gather.4.cloned.1.call-start
  7.2 1.8 convert_convert_fusion
  9.0 0.0 all-gather.4.cloned.1.call-update
  9.1 0.0 reduce-scatter.4.cloned.1.call-start
  9.1 0.7 fusion.18
  9.8 0.7 fusion.17
  10.4 19.1 %all-gather.4.cloned.1.call-done = bf16[4096,128]{1,0:T(8,128)(2,1)} async-done(((bf16[1024,128]{1,0:T(8,128)(2,1)}), bf16[4096,128]{1,0:T(8,128)(2,1)}) %all-gather.4.cloned.1.call-update) | async-done | bytes 1048592 | tf_op jit(solution)/shard_map/all_gather | solution.py:19
  29.6 7.8 %gather_fusion = bf16[128,256,128]{2,1,0:T(8,128)(2,1)} fusion(bf16[16,256,128]{2,1,0:T(8,128)(2,1)} %bitcast.39, s32[1024]{0:T(1024)S(1)} %pad_clamp_fusion), kind=kCustom, calls=%fused_computation | custom fusion | bytes 16777728 | tf_op jit(solution)/shard_map/gather | solution.py:21
  37.3 17.2 %fusion.6 = f32[128,256,128]{1,2,0:T(8,128)} fusion(bf16[128,256,128]{2,1,0:T(8,128)(2,1)} %gather_fusion, bf16[1,1,128,256,256]{4,3,2,1,0:T(8,128)(2,1)} %param.5), kind=kOutput, calls=%fused_computation.12 | convolution fusion | flops 2147483648 | bytes 41943040 | tf_op jit(solution)/shard_map/kab,kbp->kap/dot_general | solution.py:22
  54.5 17.4 %copy.11 = f32[128,256,128]{2,1,0:T(8,128)} copy(f32[128,256,128]{1,2,0:T(8,128)} %fusion.6) | data formatting | bytes 33554432 | tf_op jit(solution)/shard_map/kab,kbp->kap/dot_general | solution.py:22
  71.9 0.2 broadcast.45.clone
  72.1 0.0 copy-start
  72.1 0.0 copy-start.3
  72.1 24.3 %scatter_fusion = f32[16,256,128]{2,1,0:T(8,128)S(1)} fusion(f32[16,256,128]{2,1,0:T(8,128)S(1)} %broadcast.45.clone, s32[128]{0:T(128)S(1)} %fusion.17, f32[128,256,128]{2,1,0:T(8,128)} %copy.11), kind=kCustom, calls=%fused_computation.3 | custom fusion | flops 4194304 | bytes 50332160 | tf_op jit(solution)/shard_map/scatter-add | solution.py:26
  96.5 1.2 convert_element_type.41
  97.7 0.0 reduce-scatter.4.cloned.1.call-update
  97.7 0.0 all-gather.6.cloned.1.call-start
  97.7 27.4 %reduce-scatter.4.cloned.1.call-done = bf16[1024,128]{1,0:T(8,128)(2,1)} async-done(((bf16[4096,128]{1,0:T(8,128)(2,1)}), bf16[1024,128]{1,0:T(8,128)(2,1)}) %reduce-scatter.4.cloned.1.call-update) | async-done | bytes 262160 | tf_op jit(solution)/shard_map/reduce_scatter | solution.py:28
  125.1 1.9 fusion.15
  127.0 0.0 all-gather.6.cloned.1.call-update
  127.0 0.0 reduce-scatter.6.cloned.1.call-start
  127.0 15.5 %all-gather.6.cloned.1.call-done = bf16[4096,128]{1,0:T(8,128)(2,1)} async-done(((bf16[1024,128]{1,0:T(8,128)(2,1)}), bf16[4096,128]{1,0:T(8,128)(2,1)}) %all-gather.6.cloned.1.call-update) | async-done | bytes 1048592 | tf_op jit(solution)/shard_map/all_gather | solution.py:19
  142.5 7.8 %gather_fusion.1 = bf16[128,256,128]{2,1,0:T(8,128)(2,1)} fusion(bf16[16,256,128]{2,1,0:T(8,128)(2,1)} %bitcast.41, s32[1024]{0:T(1024)S(1)} %pad_clamp_fusion), kind=kCustom, calls=%fused_computation.1 | custom fusion | bytes 16777728 | tf_op jit(solution)/shard_map/gather | solution.py:21
  150.3 17.2 %fusion.9 = f32[128,256,128]{1,2,0:T(8,128)} fusion(bf16[128,256,128]{2,1,0:T(8,128)(2,1)} %gather_fusion.1, bf16[1,1,128,256,256]{4,3,2,1,0:T(8,128)(2,1)} %param.5), kind=kOutput, calls=%fused_computation.13 | convolution fusion | flops 2147483648 | bytes 41943040 | tf_op jit(solution)/shard_map/kab,kbp->kap/dot_general | solution.py:22
  167.4 17.4 %copy.13 = f32[128,256,128]{2,1,0:T(8,128)} copy(f32[128,256,128]{1,2,0:T(8,128)} %fusion.9) | data formatting | bytes 33554432 | tf_op jit(solution)/shard_map/kab,kbp->kap/dot_general | solution.py:22
  184.8 0.2 broadcast.45.clone.1
  185.1 24.3 %scatter_fusion.1 = f32[16,256,128]{2,1,0:T(8,128)S(1)} fusion(f32[16,256,128]{2,1,0:T(8,128)S(1)} %broadcast.45.clone.1, s32[128]{0:T(128)S(1)} %fusion.17, f32[128,256,128]{2,1,0:T(8,128)} %copy.13), kind=kCustom, calls=%fused_computation.4 | custom fusion | flops 4194304 | bytes 50332160 | tf_op jit(solution)/shard_map/scatter-add | solution.py:26
  209.4 1.2 convert_element_type.45
  210.6 0.0 reduce-scatter.6.cloned.1.call-update
  210.6 0.0 all-gather.8.cloned.1.call-start
  210.6 27.4 %reduce-scatter.6.cloned.1.call-done = bf16[1024,128]{1,0:T(8,128)(2,1)} async-done(((bf16[4096,128]{1,0:T(8,128)(2,1)}), bf16[1024,128]{1,0:T(8,128)(2,1)}) %reduce-scatter.6.cloned.1.call-update) | async-done | bytes 262160 | tf_op jit(solution)/shard_map/reduce_scatter | solution.py:28
  238.0 0.0 copy-done.1
  238.0 1.9 fusion.16
  239.9 0.0 all-gather.8.cloned.1.call-update
  240.0 0.2 reduce-scatter.8.cloned.1.call-start
  240.2 15.1 %all-gather.8.cloned.1.call-done = bf16[4096,128]{1,0:T(8,128)(2,1)} async-done(((bf16[1024,128]{1,0:T(8,128)(2,1)}), bf16[4096,128]{1,0:T(8,128)(2,1)}) %all-gather.8.cloned.1.call-update) | async-done | bytes 1048592 | tf_op jit(solution)/shard_map/all_gather | solution.py:19
  255.3 7.8 %gather_fusion.2 = bf16[128,256,128]{2,1,0:T(8,128)(2,1)} fusion(bf16[16,256,128]{2,1,0:T(8,128)(2,1)} %bitcast.40, s32[1024]{0:T(1024)S(1)} %pad_clamp_fusion), kind=kCustom, calls=%fused_computation.2 | custom fusion | bytes 16777728 | tf_op jit(solution)/shard_map/gather | solution.py:21
  263.1 17.2 %fusion.12 = f32[128,256,128]{1,2,0:T(8,128)} fusion(bf16[128,256,128]{2,1,0:T(8,128)(2,1)} %gather_fusion.2, bf16[1,1,128,256,256]{4,3,2,1,0:T(8,128)(2,1)} %param.5), kind=kOutput, calls=%fused_computation.14 | convolution fusion | flops 2147483648 | bytes 41943040 | tf_op jit(solution)/shard_map/kab,kbp->kap/dot_general | solution.py:22
  280.3 17.4 %copy.15 = f32[128,256,128]{2,1,0:T(8,128)} copy(f32[128,256,128]{1,2,0:T(8,128)} %fusion.12) | data formatting | bytes 33554432 | tf_op jit(solution)/shard_map/kab,kbp->kap/dot_general | solution.py:22
  297.7 0.2 broadcast.45
  297.9 0.0 copy-start.2
  297.9 24.3 %scatter_fusion.2 = f32[16,256,128]{2,1,0:T(8,128)S(1)} fusion(f32[16,256,128]{2,1,0:T(8,128)S(1)} %broadcast.45, s32[128]{0:T(128)S(1)} %fusion.17, f32[128,256,128]{2,1,0:T(8,128)} %copy.15), kind=kCustom, calls=%fused_computation.5 | custom fusion | flops 4194304 | bytes 50332160 | tf_op jit(solution)/shard_map/scatter-add | solution.py:26
  322.2 1.2 convert_element_type.49
  323.4 0.0 reduce-scatter.8.cloned.1.call-update
  323.4 27.4 %reduce-scatter.8.cloned.1.call-done = bf16[1024,128]{1,0:T(8,128)(2,1)} async-done(((bf16[4096,128]{1,0:T(8,128)(2,1)}), bf16[1024,128]{1,0:T(8,128)(2,1)}) %reduce-scatter.8.cloned.1.call-update) | async-done | bytes 262160 | tf_op jit(solution)/shard_map/reduce_scatter | solution.py:28
  350.9 2.2 multiply_reduce_fusion.2
  353.0 30.2 %all-reduce = (f32[1,128]{1,0:T(1,128)S(1)}, f32[1,128]{1,0:T(1,128)S(1)}, f32[1,128]{1,0:T(1,128)S(1)}) all-reduce(f32[1,128]{1,0:T(1,128)S(1)} %bitcast.47, f32[1,128]{1,0:T(1,128)S(1)} %bitcast.46, f32[1,128]{1,0:T(1,128)S(1)} %bitcast.45), channel_id=1, replica_groups=mesh['gx'=4,'gy'=4,'gz'=2] {'gx','gy'}, use_global_device_ids=true, to_apply=%region_11.0 | all-reduce | flops 384 | bytes 3072 | tf_op jit(solution)/shard_map/psum | solution.py:42
  383.3 0.6 pad_maximum_fusion
  (5 shorter events, 0.0 us)
Async XLA Ops:
  7.2 22.4 %all-gather.4.cloned.1.call-start = ((), (), s32[]{:S(2)}) async-start(), calls=%async_computation.3 | async-start | bytes 1310720 | tf_op jit(solution)/shard_map/all_gather | solution.py:19
  9.1 116.0 %reduce-scatter.4.cloned.1.call-start = ((), (), s32[]{:S(2)}) async-start(), calls=%async_computation.4 | async-start | bytes 1310720 | tf_op jit(solution)/shard_map/reduce_scatter | solution.py:28
  72.1 53.0 %copy-start = (s32[1024,128]{1,0:T(8,128)S(1)}, s32[1024,128]{1,0:T(8,128)}, u32[]{:S(2)}) copy-start(s32[1024,128]{1,0:T(8,128)} %param.8) | copy-start | bytes 1572868
  72.1 53.0 %copy-start.3 = (f32[1024]{0:T(1024)S(1)}, f32[1024]{0:T(1024)}, u32[]{:S(2)}) copy-start(f32[1024]{0:T(1024)} %param.9) | copy-start | bytes 12292
  97.7 44.8 %all-gather.6.cloned.1.call-start = ((), (), s32[]{:S(2)}) async-start(), calls=%async_computation.5 | async-start | bytes 1310720 | tf_op jit(solution)/shard_map/all_gather | solution.py:19
  127.0 111.0 %reduce-scatter.6.cloned.1.call-start = ((), (), s32[]{:S(2)}) async-start(), calls=%async_computation.6 | async-start | bytes 1310720 | tf_op jit(solution)/shard_map/reduce_scatter | solution.py:28
  185.1 53.0 %copy-start.1 = (bf16[1024,128]{1,0:T(8,128)(2,1)S(1)}, bf16[1024,128]{1,0:T(8,128)(2,1)}, u32[]{:S(2)}) copy-start(bf16[1024,128]{1,0:T(8,128)(2,1)} %reduce-scatter.4.cloned.1.call-done) | copy-start | bytes 786436
  210.6 44.7 %all-gather.8.cloned.1.call-start = ((), (), s32[]{:S(2)}) async-start(), calls=%async_computation.7 | async-start | bytes 1310720 | tf_op jit(solution)/shard_map/all_gather | solution.py:19
  240.0 110.9 %reduce-scatter.8.cloned.1.call-start = ((), (), s32[]{:S(2)}) async-start(), calls=%async_computation.8 | async-start | bytes 1310720 | tf_op jit(solution)/shard_map/reduce_scatter | solution.py:28
  297.9 53.0 %copy-start.2 = (bf16[1024,128]{1,0:T(8,128)(2,1)S(1)}, bf16[1024,128]{1,0:T(8,128)(2,1)}, u32[]{:S(2)}) copy-start(bf16[1024,128]{1,0:T(8,128)(2,1)} %reduce-scatter.6.cloned.1.call-done) | copy-start | bytes 786436
Sparse Core Ops, SparseCore 0:
  10.1 19.4 all-gather.3
  97.8 27.2 reduce-scatter.3
  127.2 15.2 all-gather.5
  210.7 27.2 reduce-scatter.5
  240.1 15.1 all-gather.7
  323.6 27.2 reduce-scatter.7
where the time goes:
time: 393 us; the launch traced here: 391 us
  waiting for transfers between devices  132 us (34%)
  other arithmetic  86.2 us (22%)
  local copies, waits for them, and re-layouts  76.1 us (19%)
  matrix products  51.5 us (13%)
  blocking collectives  30.2 us (8%)
  between operations  14.2 us (4%)
    reduce_scatter x3, waiting for transfers between devices, apply_operator(): lax.psum_scatter(partial_rows.reshape(lax.axis_size('gx') * local_rows, p...  82.1 us
    scatter-add x3, other arithmetic, apply_operator(): jnp.zeros((tile_rows, block_size, probe_count), jnp.float32).at[rows_here]  73 us
    dot_general x3, local copies, waits for them, and re-layouts, apply_operator(): jnp.einsum('kab,kbp->kap', tile_blocks, picked, preferred_element_type=jn...  52.2 us
    dot_general x3, matrix products, apply_operator(): jnp.einsum('kab,kbp->kap', tile_blocks, picked, preferred_element_type=jn...  51.5 us
    all_gather x3, waiting for transfers between devices, apply_operator(): whole = lax.all_gather(rounded, 'gy', axis=0, tiled=True)  49.7 us
    psum x1, blocking collectives, body(): lax.psum(jnp.sum(signs * term, axis=0), ('gx', 'gy'))  30.2 us
    gather x3, local copies, waits for them, and re-layouts, apply_operator(): picked = whole[cols_here]  23.3 us
  transfers between devices with their start and end apart: 6, of which 6 were waited for; matrix products, arithmetic and copies ran while one was open for 0% of the time, Pallas kernels for 0%

commit v1 on v0

--- a/solution.py
+++ b/solution.py
@@ -39,7 +39,10 @@
     second = 2.0 * apply_operator(first) - signs
     third = 2.0 * apply_operator(second) - first
     forms = jnp.stack(
-        [lax.psum(jnp.sum(signs * term, axis=0), ("gx", "gy")) for term in (first, second, third)]
+        [
+            lax.psum(lax.psum(jnp.sum(signs * term, axis=0), "gy"), "gx")
+            for term in (first, second, third)
+        ]
     )
     return (forms, third)
 

time: 393 us -> 378 us (0.962)
  blocking collectives: 30.2 us -> 15.3 us
    psum x1 -> x2, blocking collectives: 30.2 us -> 15.3 us  [the longest x1 9.16 us: body(): lax.psum(lax.psum(jnp.sum(signs * term, axis=0), 'gy'), 'gx')]
where the time goes in v1:
time: 378 us; the launch traced here: 376 us
  waiting for transfers between devices  132 us (35%)
  other arithmetic  86.2 us (23%)
  local copies, waits for them, and re-layouts  76.1 us (20%)
  matrix products  51.5 us (14%)
  blocking collectives  15.3 us (4%)
  between operations  14.2 us (4%)
    reduce_scatter x3, waiting for transfers between devices, apply_operator(): lax.psum_scatter(partial_rows.reshape(lax.axis_size('gx') * local_rows, p...  82.1 us
    scatter-add x3, other arithmetic, apply_operator(): jnp.zeros((tile_rows, block_size, probe_count), jnp.float32).at[rows_here]  73 us
    dot_general x3, local copies, waits for them, and re-layouts, apply_operator(): jnp.einsum('kab,kbp->kap', tile_blocks, picked, preferred_element_type=jn...  52.2 us
    dot_general x3, matrix products, apply_operator(): jnp.einsum('kab,kbp->kap', tile_blocks, picked, preferred_element_type=jn...  51.5 us
    all_gather x3, waiting for transfers between devices, apply_operator(): whole = lax.all_gather(rounded, 'gy', axis=0, tiled=True)  49.7 us
    gather x3, local copies, waits for them, and re-layouts, apply_operator(): picked = whole[cols_here]  23.3 us
    psum x1, blocking collectives, body(): lax.psum(lax.psum(jnp.sum(signs * term, axis=0), 'gy'), 'gx')  9.16 us
  transfers between devices with their start and end apart: 6, of which 6 were waited for; matrix products, arithmetic and copies ran while one was open for 0% of the time, Pallas kernels for 0%

profile of v1, /device:TPU:0, one launch (start us, length us, event | category | flops | bytes accessed | tf_op | source)
XLA Modules:
  0.0 375.8 jit_solution(4294106083529665687)
XLA Ops:
  7.2 0.0 all-gather.4.cloned.1.call-start
  7.2 1.8 convert_convert_fusion
  9.0 0.0 all-gather.4.cloned.1.call-update
  9.1 0.0 reduce-scatter.4.cloned.1.call-start
  9.1 0.7 fusion.18
  9.8 0.7 fusion.17
  10.4 19.1 %all-gather.4.cloned.1.call-done = bf16[4096,128]{1,0:T(8,128)(2,1)} async-done(((bf16[1024,128]{1,0:T(8,128)(2,1)}), bf16[4096,128]{1,0:T(8,128)(2,1)}) %all-gather.4.cloned.1.call-update) | async-done | bytes 1048592 | tf_op jit(solution)/shard_map/all_gather | solution.py:19
  29.6 7.8 %gather_fusion = bf16[128,256,128]{2,1,0:T(8,128)(2,1)} fusion(bf16[16,256,128]{2,1,0:T(8,128)(2,1)} %bitcast.39, s32[1024]{0:T(1024)S(1)} %pad_clamp_fusion), kind=kCustom, calls=%fused_computation | custom fusion | bytes 16777728 | tf_op jit(solution)/shard_map/gather | solution.py:21
  37.3 17.2 %fusion.6 = f32[128,256,128]{1,2,0:T(8,128)} fusion(bf16[128,256,128]{2,1,0:T(8,128)(2,1)} %gather_fusion, bf16[1,1,128,256,256]{4,3,2,1,0:T(8,128)(2,1)} %param.5), kind=kOutput, calls=%fused_computation.12 | convolution fusion | flops 2147483648 | bytes 41943040 | tf_op jit(solution)/shard_map/kab,kbp->kap/dot_general | solution.py:22
  54.5 17.4 %copy.11 = f32[128,256,128]{2,1,0:T(8,128)} copy(f32[128,256,128]{1,2,0:T(8,128)} %fusion.6) | data formatting | bytes 33554432 | tf_op jit(solution)/shard_map/kab,kbp->kap/dot_general | solution.py:22
  71.9 0.2 broadcast.45.clone
  72.1 0.0 copy-start
  72.1 0.0 copy-start.3
  72.1 24.3 %scatter_fusion = f32[16,256,128]{2,1,0:T(8,128)S(1)} fusion(f32[16,256,128]{2,1,0:T(8,128)S(1)} %broadcast.45.clone, s32[128]{0:T(128)S(1)} %fusion.17, f32[128,256,128]{2,1,0:T(8,128)} %copy.11), kind=kCustom, calls=%fused_computation.3 | custom fusion | flops 4194304 | bytes 50332160 | tf_op jit(solution)/shard_map/scatter-add | solution.py:26
  96.5 1.2 convert_element_type.41
  97.7 0.0 reduce-scatter.4.cloned.1.call-update
  97.7 0.0 all-gather.6.cloned.1.call-start
  97.7 27.4 %reduce-scatter.4.cloned.1.call-done = bf16[1024,128]{1,0:T(8,128)(2,1)} async-done(((bf16[4096,128]{1,0:T(8,128)(2,1)}), bf16[1024,128]{1,0:T(8,128)(2,1)}) %reduce-scatter.4.cloned.1.call-update) | async-done | bytes 262160 | tf_op jit(solution)/shard_map/reduce_scatter | solution.py:28
  125.1 1.9 fusion.15
  127.0 0.0 all-gather.6.cloned.1.call-update
  127.0 0.0 reduce-scatter.6.cloned.1.call-start
  127.0 15.5 %all-gather.6.cloned.1.call-done = bf16[4096,128]{1,0:T(8,128)(2,1)} async-done(((bf16[1024,128]{1,0:T(8,128)(2,1)}), bf16[4096,128]{1,0:T(8,128)(2,1)}) %all-gather.6.cloned.1.call-update) | async-done | bytes 1048592 | tf_op jit(solution)/shard_map/all_gather | solution.py:19
  142.5 7.8 %gather_fusion.1 = bf16[128,256,128]{2,1,0:T(8,128)(2,1)} fusion(bf16[16,256,128]{2,1,0:T(8,128)(2,1)} %bitcast.41, s32[1024]{0:T(1024)S(1)} %pad_clamp_fusion), kind=kCustom, calls=%fused_computation.1 | custom fusion | bytes 16777728 | tf_op jit(solution)/shard_map/gather | solution.py:21
  150.3 17.2 %fusion.9 = f32[128,256,128]{1,2,0:T(8,128)} fusion(bf16[128,256,128]{2,1,0:T(8,128)(2,1)} %gather_fusion.1, bf16[1,1,128,256,256]{4,3,2,1,0:T(8,128)(2,1)} %param.5), kind=kOutput, calls=%fused_computation.13 | convolution fusion | flops 2147483648 | bytes 41943040 | tf_op jit(solution)/shard_map/kab,kbp->kap/dot_general | solution.py:22
  167.4 17.4 %copy.13 = f32[128,256,128]{2,1,0:T(8,128)} copy(f32[128,256,128]{1,2,0:T(8,128)} %fusion.9) | data formatting | bytes 33554432 | tf_op jit(solution)/shard_map/kab,kbp->kap/dot_general | solution.py:22
  184.8 0.2 broadcast.45.clone.1
  185.1 24.3 %scatter_fusion.1 = f32[16,256,128]{2,1,0:T(8,128)S(1)} fusion(f32[16,256,128]{2,1,0:T(8,128)S(1)} %broadcast.45.clone.1, s32[128]{0:T(128)S(1)} %fusion.17, f32[128,256,128]{2,1,0:T(8,128)} %copy.13), kind=kCustom, calls=%fused_computation.4 | custom fusion | flops 4194304 | bytes 50332160 | tf_op jit(solution)/shard_map/scatter-add | solution.py:26
  209.4 1.2 convert_element_type.45
  210.6 0.0 reduce-scatter.6.cloned.1.call-update
  210.6 0.0 all-gather.8.cloned.1.call-start
  210.6 27.4 %reduce-scatter.6.cloned.1.call-done = bf16[1024,128]{1,0:T(8,128)(2,1)} async-done(((bf16[4096,128]{1,0:T(8,128)(2,1)}), bf16[1024,128]{1,0:T(8,128)(2,1)}) %reduce-scatter.6.cloned.1.call-update) | async-done | bytes 262160 | tf_op jit(solution)/shard_map/reduce_scatter | solution.py:28
  238.0 0.0 copy-done.1
  238.0 1.9 fusion.16
  239.9 0.0 all-gather.8.cloned.1.call-update
  240.0 0.2 reduce-scatter.8.cloned.1.call-start
  240.2 15.1 %all-gather.8.cloned.1.call-done = bf16[4096,128]{1,0:T(8,128)(2,1)} async-done(((bf16[1024,128]{1,0:T(8,128)(2,1)}), bf16[4096,128]{1,0:T(8,128)(2,1)}) %all-gather.8.cloned.1.call-update) | async-done | bytes 1048592 | tf_op jit(solution)/shard_map/all_gather | solution.py:19
  255.3 7.8 %gather_fusion.2 = bf16[128,256,128]{2,1,0:T(8,128)(2,1)} fusion(bf16[16,256,128]{2,1,0:T(8,128)(2,1)} %bitcast.40, s32[1024]{0:T(1024)S(1)} %pad_clamp_fusion), kind=kCustom, calls=%fused_computation.2 | custom fusion | bytes 16777728 | tf_op jit(solution)/shard_map/gather | solution.py:21
  263.1 17.2 %fusion.12 = f32[128,256,128]{1,2,0:T(8,128)} fusion(bf16[128,256,128]{2,1,0:T(8,128)(2,1)} %gather_fusion.2, bf16[1,1,128,256,256]{4,3,2,1,0:T(8,128)(2,1)} %param.5), kind=kOutput, calls=%fused_computation.14 | convolution fusion | flops 2147483648 | bytes 41943040 | tf_op jit(solution)/shard_map/kab,kbp->kap/dot_general | solution.py:22
  280.3 17.4 %copy.15 = f32[128,256,128]{2,1,0:T(8,128)} copy(f32[128,256,128]{1,2,0:T(8,128)} %fusion.12) | data formatting | bytes 33554432 | tf_op jit(solution)/shard_map/kab,kbp->kap/dot_general | solution.py:22
  297.7 0.2 broadcast.45
  297.9 24.3 %scatter_fusion.2 = f32[16,256,128]{2,1,0:T(8,128)S(1)} fusion(f32[16,256,128]{2,1,0:T(8,128)S(1)} %broadcast.45, s32[128]{0:T(128)S(1)} %fusion.17, f32[128,256,128]{2,1,0:T(8,128)} %copy.15), kind=kCustom, calls=%fused_computation.5 | custom fusion | flops 4194304 | bytes 50332160 | tf_op jit(solution)/shard_map/scatter-add | solution.py:26
  322.2 1.2 convert_element_type.49
  323.4 0.0 reduce-scatter.8.cloned.1.call-update
  323.4 27.4 %reduce-scatter.8.cloned.1.call-done = bf16[1024,128]{1,0:T(8,128)(2,1)} async-done(((bf16[4096,128]{1,0:T(8,128)(2,1)}), bf16[1024,128]{1,0:T(8,128)(2,1)}) %reduce-scatter.8.cloned.1.call-update) | async-done | bytes 262160 | tf_op jit(solution)/shard_map/reduce_scatter | solution.py:28
  350.9 2.2 multiply_reduce_fusion.2
  353.0 6.2 %all-reduce = (f32[128]{0:T(128)S(1)}, f32[128]{0:T(128)S(1)}, f32[128]{0:T(128)S(1)}) all-reduce(f32[128]{0:T(128)S(1)} %get-tuple-element.4, f32[128]{0:T(128)S(1)} %get-tuple-element.3, f32[128]{0:T(128)S(1)} %get-tuple-element.2), channel_id=1, replica_groups=mesh['gx'=4,'gy'=4,'gz'=2] {'gy'}, use_global_device_ids=true, to_apply=%region_13.0 | all-reduce | flops 384 | bytes 3072 | tf_op jit(solution)/shard_map/psum | solution.py:43
  359.2 9.2 %all-reduce.1 = (f32[1,128]{1,0:T(1,128)S(1)}, f32[1,128]{1,0:T(1,128)S(1)}, f32[1,128]{1,0:T(1,128)S(1)}) all-reduce(f32[1,128]{1,0:T(1,128)S(1)} %bitcast.45, f32[1,128]{1,0:T(1,128)S(1)} %bitcast.46, f32[1,128]{1,0:T(1,128)S(1)} %bitcast.47), channel_id=1, replica_groups=mesh['gx'=4,'gy'=4,'gz'=2] {'gx'}, use_global_device_ids=true, to_apply=%region_14.0 | all-reduce | flops 384 | bytes 3072 | tf_op jit(solution)/shard_map/psum | solution.py:43
  368.4 0.6 pad_maximum_fusion
  (6 shorter events, 0.0 us)
Async XLA Ops:
  7.2 22.4 %all-gather.4.cloned.1.call-start = ((), (), s32[]{:S(2)}) async-start(), calls=%async_computation.3 | async-start | bytes 1310720 | tf_op jit(solution)/shard_map/all_gather | solution.py:19
  9.1 116.0 %reduce-scatter.4.cloned.1.call-start = ((), (), s32[]{:S(2)}) async-start(), calls=%async_computation.4 | async-start | bytes 1310720 | tf_op jit(solution)/shard_map/reduce_scatter | solution.py:28
  72.1 53.0 %copy-start = (s32[1024,128]{1,0:T(8,128)S(1)}, s32[1024,128]{1,0:T(8,128)}, u32[]{:S(2)}) copy-start(s32[1024,128]{1,0:T(8,128)} %param.8) | copy-start | bytes 1572868
  72.1 53.0 %copy-start.3 = (f32[1024]{0:T(1024)S(1)}, f32[1024]{0:T(1024)}, u32[]{:S(2)}) copy-start(f32[1024]{0:T(1024)} %param.9) | copy-start | bytes 12292
  97.7 44.8 %all-gather.6.cloned.1.call-start = ((), (), s32[]{:S(2)}) async-start(), calls=%async_computation.5 | async-start | bytes 1310720 | tf_op jit(solution)/shard_map/all_gather | solution.py:19
  127.0 111.0 %reduce-scatter.6.cloned.1.call-start = ((), (), s32[]{:S(2)}) async-start(), calls=%async_computation.6 | async-start | bytes 1310720 | tf_op jit(solution)/shard_map/reduce_scatter | solution.py:28
  185.1 53.0 %copy-start.1 = (bf16[1024,128]{1,0:T(8,128)(2,1)S(1)}, bf16[1024,128]{1,0:T(8,128)(2,1)}, u32[]{:S(2)}) copy-start(bf16[1024,128]{1,0:T(8,128)(2,1)} %reduce-scatter.4.cloned.1.call-done) | copy-start | bytes 786436
  210.6 44.7 %all-gather.8.cloned.1.call-start = ((), (), s32[]{:S(2)}) async-start(), calls=%async_computation.7 | async-start | bytes 1310720 | tf_op jit(solution)/shard_map/all_gather | solution.py:19
  240.0 110.9 %reduce-scatter.8.cloned.1.call-start = ((), (), s32[]{:S(2)}) async-start(), calls=%async_computation.8 | async-start | bytes 1310720 | tf_op jit(solution)/shard_map/reduce_scatter | solution.py:28
  297.9 53.0 %copy-start.2 = (bf16[1024,128]{1,0:T(8,128)(2,1)S(1)}, bf16[1024,128]{1,0:T(8,128)(2,1)}, u32[]{:S(2)}) copy-start(bf16[1024,128]{1,0:T(8,128)(2,1)} %reduce-scatter.6.cloned.1.call-done) | copy-start | bytes 786436
Sparse Core Ops, SparseCore 0:
  10.1 19.4 all-gather.3
  97.8 27.2 reduce-scatter.3
  127.2 15.2 all-gather.5
  210.7 27.2 reduce-scatter.5
  240.1 15.1 all-gather.7
  323.6 27.2 reduce-scatter.7
